TPU v7x, 32 devices: a whole 2x2x4 slice. The times are simulated.
32 devices in a mesh: pairs: 8 (over z, y), cols: 4 (over x, core).
Axes of the slice: x: 2, y: 2, z: 4, core: 2. Of those that a mesh axis runs over, the one named last changes fastest.
Arguments:
- amplitudes: bfloat16 [64, 256, 256], P('pairs', 'cols'), may hold values from -6 to 6
- pno_counts: int32 [64], P('pairs'), may hold values from 96 to 256
- fock_blocks: bfloat16 [64, 256, 256], P('pairs'), may hold values from -1 to 5, as said below
- exchange_blocks: bfloat16 [64, 256, 256], P('pairs', 'cols'), may hold values from -6 to 6
- intersections: bfloat16 [64, 32, 256, 256], P('pairs', None, 'cols'), may hold values from -0.375 to 0.375
- partners: int32 [64, 32], P('pairs'), may hold values from 0 to 63, as said below
- couplings: float32 [64, 32], P('pairs'), may hold values from -3 to 3
Outputs:
- residual_blocks: bfloat16 [64, 256, 256], P('pairs', 'cols')
Inputs may be any that keep to these rules, and one draw needn't show every extreme that they name: `partners`: within the coupling lists of one aligned block of 8 pairs, at most 64 entries name pairs of any one aligned block of 8 pairs, and exactly 64 do for some block. `fock_blocks`: each block is symmetric.
All inputs are finite; a program needn't handle non-finite values.
Results may differ from a plain program's by a relative error of at most 0.0022.
Values may be sent and summed in bfloat16 or wider, within the bound.
No kernel may reach another device: no remote copies, remote signals or barrier semaphores. Data moves between devices by JAX's collectives and lax.ppermute only.
A program may use at most 128 MiB of HBM per device.

v0:
```python
import jax
import jax.numpy as jnp
from jax import lax
from jax.sharding import PartitionSpec as P

CPL = 32


def shards(
    amplitudes, pno_counts, fock_blocks, exchange_blocks, intersections, partners, couplings
):
    local_pairs, share, width = amplitudes.shape
    column = lax.axis_index("cols")
    row_keep = column * share + jnp.arange(share, dtype=jnp.int32)[None, :] < pno_counts[:, None]
    col_keep = jnp.arange(width, dtype=jnp.int32)[None, :] < pno_counts[:, None]
    keep = row_keep[:, :, None] & col_keep[:, None, :]
    masked = jnp.where(keep, amplitudes, jnp.zeros_like(amplitudes))
    linear = partners.reshape(-1)
    empty = jnp.zeros((local_pairs * CPL, share, width), jnp.bfloat16)
    piece = lax.all_gather(masked, "pairs", axis=0, tiled=True)
    present = (linear >= 0) & (linear < piece.shape[0])
    picked = piece[jnp.clip(linear, 0, piece.shape[0] - 1)]
    partner_flat = jnp.where(present[:, None, None], picked, empty)
    partner_blocks = partner_flat.reshape(local_pairs, CPL, share, width)
    fock_cols = lax.dynamic_slice_in_dim(fock_blocks, column * share, share, 2)
    partial_value = jnp.einsum(
        "pab,pbc->pac", fock_cols, masked, preferred_element_type=jnp.float32
    )
    whole_intersections = lax.all_gather(intersections, "cols", axis=2, tiled=True)
    projected = jnp.einsum(
        "pqab,pqbc->pqac", partner_blocks, whole_intersections, preferred_element_type=jnp.float32
    ).astype(jnp.bfloat16)
    for slot_index in range(CPL):
        term = jnp.einsum(
            "pcd,pca->pda",
            intersections[:, slot_index],
            projected[:, slot_index],
            preferred_element_type=jnp.float32,
        )
        partial_value = partial_value + couplings[:, slot_index, None, None] * term
    summed = lax.psum_scatter(partial_value, "cols", scatter_dimension=1, tiled=True)
    fock_term = jnp.einsum("pab,pbc->pac", masked, fock_blocks, preferred_element_type=jnp.float32)
    total = exchange_blocks.astype(jnp.float32) + fock_term + summed
    return jnp.where(keep, total, jnp.zeros_like(total)).astype(jnp.bfloat16)


def solution(mesh):
    in_specs = (
        P("pairs", "cols", None),
        P("pairs"),
        P("pairs", None, None),
        P("pairs", "cols", None),
        P("pairs", None, "cols", None),
        P("pairs", None),
        P("pairs", None),
    )
    out_specs = P("pairs", "cols", None)
    return jax.shard_map(shards, mesh=mesh, in_specs=in_specs, out_specs=out_specs, check_vma=False)
```

profile of v0, /device:TPU:0, one launch (start us, length us, event | category | flops | bytes accessed | tf_op | source)
XLA Modules:
  0.0 406.6 jit_solution(1802354815083428256)
XLA Ops:
  6.5 0.8 iota_compare_fusion
  7.4 0.7 broadcast_compare_fusion
  8.1 1.8 and_select_fusion
  9.9 0.0 all-gather.5.cloned.1.call-start
  10.0 0.7 all-gather.5.cloned.1.call-update
  10.7 0.0 reduce-scatter.2.cloned.1.call-start
  10.8 0.1 min.12
  10.9 0.4 slice_reduce_fusion.30
  11.3 0.5 slice_reduce_fusion.31
  11.7 50.1 %all-gather.3.cloned.1.call-done = bf16[64,64,256]{2,1,0:T(8,128)(2,1)} async-done(((bf16[8,64,256]{2,1,0:T(8,128)(2,1)}), bf16[64,64,256]{2,1,0:T(8,128)(2,1)}) %all-gather.3.cloned.1.call-update) | async-done | bytes 2097168 | tf_op jit(solution)/shard_map/all_gather | solution.py:20
  61.9 12.4 %gather_fusion = bf16[256,64,256]{2,1,0:T(8,128)(2,1)} fusion(bf16[64,64,256]{2,1,0:T(8,128)(2,1)} %all-gather.3.cloned.1.call-done, s32[1024]{0:T(1024)S(1)} %pad_clamp_fusion), kind=kCustom, calls=%fused_computation | custom fusion | bytes 16778240 | tf_op jit(solution)/shard_map/gather | solution.py:22
  74.2 189.3 %all-gather.5.cloned.1.call-done = bf16[8,32,256,256]{3,2,1,0:T(8,128)(2,1)} async-done(((bf16[8,32,64,256]{3,2,1,0:T(8,128)(2,1)}), bf16[8,32,256,256]{3,2,1,0:T(8,128)(2,1)}) %all-gather.5.cloned.1.call-update) | async-done | bytes 33554448 | tf_op jit(solution)/shard_map/all_gather | solution.py:29
  263.5 15.6 %fusion.3 = bf16[8,32,64,256]{3,2,1,0:T(8,128)(2,1)S(1)} fusion(bf16[8,32,256,256]{3,2,1,0:T(8,128)(2,1)} %all-gather.5.cloned.1.call-done, bf16[8,32,64,256]{3,2,1,0:T(8,128)(2,1)} %bitcast.390, pred[8,32]{1,0:T(8,128)(4,1)S(1)} %compare_and_fusion), kind=kOutput, calls=%fused_computation.4 | convolution fusion | flops 2155872256 | bytes 50331904 | tf_op jit(solution)/shard_map/pqab,pqbc->pqac/dot_general | solution.py:30
  279.1 2.9 fusion.11
  282.0 2.8 fusion.12
  284.8 2.7 fusion.13
  287.6 2.9 fusion.14
  290.5 2.8 fusion.15
  293.3 2.8 fusion.16
  296.1 1.8 fusion.17
  297.9 1.9 fusion.18
  299.7 1.8 fusion.19
  301.6 1.8 fusion.20
  303.4 1.8 fusion.21
  305.2 1.8 fusion.22
  307.0 1.8 fusion.23
  308.8 1.9 fusion.24
  310.7 1.8 fusion.25
  312.5 1.8 fusion.26
  314.3 1.8 fusion.27
  316.1 1.8 fusion.28
  317.9 1.9 fusion.29
  319.8 1.8 fusion.30
  321.6 1.8 fusion.31
  323.4 1.8 fusion.32
  325.2 1.8 fusion.33
  327.0 1.8 fusion.34
  328.8 1.8 fusion.35
  330.6 1.8 fusion.36
  332.4 1.9 fusion.37
  334.3 1.8 fusion.38
  336.1 1.8 fusion.39
  337.9 1.8 fusion.40
  339.7 1.8 fusion.41
  341.5 1.8 fusion.42
  343.3 23.3 %bitcast_add_fusion = f32[8,256,256]{2,1,0:T(8,128)} fusion(f32[8,256,256]{1,2,0:T(8,128)} %fusion.11, f32[8,256,256]{1,2,0:T(8,128)} %fusion.12, f32[8,256,256]{1,2,0:T(8,128)} %fusion.13, f32[8,256,256]{1,2,0:T(8,128)} %fusion.14, f32[8,256,256]{1,2,0:T(8,128)} %fusion.15, f32[8,256,256]{1,2,0:T(8,128)} %fusion.16, f32[8,256,256]{1,2,0:T(8,128)} %fusion.17, ...), kind=kOutput, calls=%fused_computation.6 | convolution fusion | flops 100663296 | bytes 70008832 | tf_op jit(solution)/shard_map/pab,pbc->pac/dot_general | solution.py:26
  366.7 31.3 %reduce-scatter.2.cloned.1.call-done = f32[8,64,256]{2,1,0:T(8,128)} async-done(((f32[8,256,256]{2,1,0:T(8,128)}), f32[8,64,256]{2,1,0:T(8,128)}) %reduce-scatter.2.cloned.1.call-update) | async-done | bytes 524304 | tf_op jit(solution)/shard_map/reduce_scatter | solution.py:41
  398.0 2.1 fusion.9
  (23 shorter events, 0.1 us)
Async XLA Ops:
  6.5 336.8 %copy-start = (bf16[8,256,256]{2,1,0:T(8,128)(2,1)S(1)}, bf16[8,256,256]{2,1,0:T(8,128)(2,1)}, u32[]{:S(2)}) copy-start(bf16[8,256,256]{2,1,0:T(8,128)(2,1)} %param.9) | copy-start | bytes 3145732
  6.5 55.3 %all-gather.3.cloned.1.call-start = ((), (), s32[]{:S(2)}) async-start(), calls=%async_computation.1 | async-start | bytes 2359296 | tf_op jit(solution)/shard_map/all_gather | solution.py:20
  9.9 0.8 copy-start.4
  9.9 0.9 copy-start.2
  9.9 253.6 %all-gather.5.cloned.1.call-start = ((), (), s32[]{:S(2)}) async-start(), calls=%async_computation.2 | async-start | bytes 41943040 | tf_op jit(solution)/shard_map/all_gather | solution.py:29
  10.7 387.3 %reduce-scatter.2.cloned.1.call-start = ((), (), s32[]{:S(2)}) async-start(), calls=%async_computation.3 | async-start | bytes 2621440 | tf_op jit(solution)/shard_map/reduce_scatter | solution.py:41
  279.1 17.0 %slice-start = ((s8[8388608]{0:T(1024)(128)(4,1)}), s8[4194304]{0:T(1024)(128)(4,1)S(1)}, s32[]{:S(2)}) async-start(s8[8388608]{0:T(1024)(128)(4,1)} %bitcast.388), calls=%async_computation.4 | async-start | bytes 8388608
  287.6 8.5 %slice-start.1 = ((s8[8388608]{0:T(1024)(128)(4,1)}), s8[4194304]{0:T(1024)(128)(4,1)S(1)}, s32[]{:S(2)}) async-start(s8[8388608]{0:T(1024)(128)(4,1)} %bitcast.388), calls=%async_computation.5 | async-start | bytes 8388608
  339.7 3.6 copy-start.1
  366.6 31.3 %copy-start.3 = (bf16[8,64,256]{2,1,0:T(8,128)(2,1)S(1)}, bf16[8,64,256]{2,1,0:T(8,128)(2,1)}, u32[]{:S(2)}) copy-start(bf16[8,64,256]{2,1,0:T(8,128)(2,1)} %param.10) | copy-start | bytes 786436
Sparse Core Ops, SparseCore 0:
  10.0 51.7 all-gather.2
  63.4 200.0 all-gather.4
  366.8 31.1 reduce-scatter.1
where the time goes:
time: 407 us
  waiting for transfers between devices  271 us (67%)
  matrix products  105 us (26%)
  local copies, waits for them, and re-layouts  13.4 us (3%)
  between operations  13.2 us (3%)
    all_gather x1, waiting for transfers between devices, shards(): lax.all_gather(intersections, 'cols', axis=2, tiled=True)  189 us
    dot_general x32, matrix products, shards(): jnp.einsum('pcd,pca->pda', intersections[:, slot_index], projected[:, slo...  64.2 us
    all_gather x1, waiting for transfers between devices, shards(): piece = lax.all_gather(masked, 'pairs', axis=0, tiled=True)  50.1 us
    reduce_scatter x1, waiting for transfers between devices, shards(): lax.psum_scatter(partial_value, 'cols', scatter_dimension=1, tiled=True)  31.3 us
    dot_general x1, matrix products, shards(): jnp.einsum('pab,pbc->pac', fock_cols, masked, preferred_element_type=jnp....  23.3 us
    dot_general x1, matrix products, shards(): jnp.einsum('pqab,pqbc->pqac', partner_blocks, whole_intersections, prefer...  15.6 us
    gather x1, local copies, waits for them, and re-layouts, shards(): picked = piece[jnp.clip(linear, 0, piece.shape[0] - 1)]  12.4 us
  transfers between devices with their start and end apart: 3, of which 3 were waited for; matrix products, arithmetic and copies ran while one was open for 3% of the time, Pallas kernels for 0%

commit v1 on v0

--- a/solution.py
+++ b/solution.py
@@ -4,6 +4,22 @@
 from jax.sharding import PartitionSpec as P
 
 CPL = 32
+
+
+def product_in_turn(x, axis, dim, product):
+    peers, index, rows = (lax.axis_size(axis), lax.axis_index(axis), x.shape[dim])
+    upward = [(i, (i + 1) % peers) for i in range(peers)]
+    left = [(i, (i - 1) % peers) for i in range(peers)]
+    halfway = peers // 2
+    from_left = from_right = x
+    subtotal = product(x, index * rows)
+    for hop in range(1, halfway + 1):
+        from_left = lax.ppermute(from_left, axis, upward)
+        if hop < peers - halfway:
+            from_right = lax.ppermute(from_right, axis, left)
+            subtotal = subtotal + product(from_right, (index + hop) % peers * rows)
+        subtotal = subtotal + product(from_left, (index - hop) % peers * rows)
+    return subtotal
 
 
 def shards(
@@ -26,9 +42,16 @@
     partial_value = jnp.einsum(
         "pab,pbc->pac", fock_cols, masked, preferred_element_type=jnp.float32
     )
-    whole_intersections = lax.all_gather(intersections, "cols", axis=2, tiled=True)
-    projected = jnp.einsum(
-        "pqab,pqbc->pqac", partner_blocks, whole_intersections, preferred_element_type=jnp.float32
+    projected = product_in_turn(
+        intersections,
+        "cols",
+        2,
+        lambda shard, offset: jnp.einsum(
+            "pqab,pqbc->pqac",
+            lax.dynamic_slice_in_dim(partner_blocks, offset, shard.shape[2], axis=3),
+            shard,
+            preferred_element_type=jnp.float32,
+        ),
     ).astype(jnp.bfloat16)
     for slot_index in range(CPL):
         term = jnp.einsum(

time: 407 us -> 436 us (1.071)
  matrix products: 105 us -> 149 us
  waiting for transfers between devices: 271 us -> 243 us
  other arithmetic: 3.37 us -> 12 us
  starting transfers between devices: 0.08 us -> 4.97 us
    ppermute x0 -> x3, waiting for transfers between devices: none -> 208 us  [the longest x2 208 us: product_in_turn(): from_left = lax.ppermute(from_left, axis, upward)]
    all_gather x1 -> x0, waiting for transfers between devices: 189 us -> none  [shards(): lax.all_gather(intersections, 'cols', axis=2, tiled=True)]
    all_gather x1, waiting for transfers between devices: 50.1 us -> 0.01 us  [shards(): piece = lax.all_gather(masked, 'pairs', axis=0, tiled=True)]
    dot_general x1 -> x4, matrix products: 15.6 us -> 60.4 us  [shards(): jnp.einsum('pqab,pqbc->pqac', lax.dynamic_slice_in_dim(partner_blocks, of...]
    select_n x0 -> x1, other arithmetic: none -> 7.32 us  [shards(): partner_flat = jnp.where(present[:, None, None], picked, empty)]
    ppermute x0 -> x3, starting transfers between devices: none -> 4.93 us  [the longest x2 3.01 us: product_in_turn(): from_left = lax.ppermute(from_left, axis, upward)]
  transfers between devices with their start and end apart: 3 -> 5, of which waited for: 3 -> 3; matrix products, arithmetic and copies ran while one was open for 3% -> 14% of each run, Pallas kernels for 0% -> 0%
where the time goes in v1:
time: 436 us
  waiting for transfers between devices  243 us (56%)
  matrix products  149 us (34%)
  local copies, waits for them, and re-layouts  13.8 us (3%)
  between operations  13.5 us (3%)
  other arithmetic  12 us (3%)
  starting transfers between devices  4.97 us (1%)
    ppermute x2, waiting for transfers between devices, product_in_turn(): from_left = lax.ppermute(from_left, axis, upward)  208 us
    dot_general x32, matrix products, shards(): jnp.einsum('pcd,pca->pda', intersections[:, slot_index], projected[:, slo...  64.2 us
    dot_general x4, matrix products, shards(): jnp.einsum('pqab,pqbc->pqac', lax.dynamic_slice_in_dim(partner_blocks, of...  60.4 us
    reduce_scatter x1, waiting for transfers between devices, shards(): lax.psum_scatter(partial_value, 'cols', scatter_dimension=1, tiled=True)  35.2 us
    dot_general x1, matrix products, shards(): jnp.einsum('pab,pbc->pac', fock_cols, masked, preferred_element_type=jnp....  22.2 us
    gather x1, local copies, waits for them, and re-layouts, shards(): picked = piece[jnp.clip(linear, 0, piece.shape[0] - 1)]  10.2 us
  transfers between devices with their start and end apart: 5, of which 3 were waited for; matrix products, arithmetic and copies ran while one was open for 14% of the time, Pallas kernels for 0%

profile of v1, /device:TPU:0, one launch (start us, length us, event | category | flops | bytes accessed | tf_op | source)
XLA Modules:
  0.0 435.7 jit_solution(9594796857403258096)
XLA Ops:
  7.0 1.9 collective-permute-start
  10.4 1.8 and_select_fusion
  12.3 175.4 %collective-permute-done.1 = bf16[8,32,64,256]{3,2,1,0:T(8,128)(2,1)} collective-permute-done((bf16[8,32,64,256]{3,2,1,0:T(8,128)(2,1)}, bf16[8,32,64,256]{3,2,1,0:T(8,128)(2,1)}, u32[]{:S(2)}, u32[]{:S(2)}) %collective-permute-start.1) | collective-permute-done | bytes 8388640 | tf_op jit(solution)/shard_map/ppermute | solution.py:17
  187.7 2.5 collective-permute-start.2
  191.0 1.6 slice_reduce_fusion.30
  192.5 1.9 slice_reduce_fusion.31
  195.2 10.2 %gather_fusion = bf16[256,64,256]{2,1,0:T(8,128)(2,1)} fusion(bf16[64,64,256]{2,1,0:T(8,128)(2,1)} %all-gather.2.cloned.1.call-done, s32[1024]{0:T(1024)S(1)} %pad_clamp_fusion), kind=kCustom, calls=%fused_computation | custom fusion | bytes 16778240 | tf_op jit(solution)/shard_map/gather | solution.py:38
  205.4 7.3 %broadcast_select_fusion = bf16[8,32,64,256]{3,2,1,0:T(8,128)(2,1)} fusion(bf16[8,32,64,256]{3,2,1,0:T(8,128)(2,1)} %bitcast.393, pred[8,32]{1,0:T(8,128)(4,1)S(1)} %compare_and_fusion), kind=kLoop, calls=%fused_computation.2 | loop fusion | flops 4194304 | bytes 16777472 | tf_op jit(solution)/shard_map/jit(_where)/select_n | solution.py:39
  212.7 12.9 %fusion.5 = f32[8,32,64,256]{3,2,1,0:T(8,128)} fusion(bf16[8,32,64,256]{3,2,1,0:T(8,128)(2,1)} %param.11, bf16[8,32,64,256]{3,2,1,0:T(8,128)(2,1)} %broadcast_select_fusion, s32[]{:T(128)S(6)} %select_n.52), kind=kOutput, calls=%fused_computation.8 | convolution fusion | flops 536870912 | bytes 29360132 | tf_op jit(solution)/shard_map/pqab,pqbc->pqac/dot_general | solution.py:49
  225.6 11.6 %fusion.1 = f32[8,32,64,256]{3,2,1,0:T(8,128)} fusion(bf16[8,32,64,256]{3,2,1,0:T(8,128)(2,1)} %collective-permute-done.1, bf16[8,32,64,256]{3,2,1,0:T(8,128)(2,1)S(1)} %copy-done.1, s32[]{:T(128)S(6)} %select_n.58), kind=kOutput, calls=%fused_computation.4 | convolution fusion | flops 536870912 | bytes 29360132 | tf_op jit(solution)/shard_map/pqab,pqbc->pqac/dot_general | solution.py:49
  237.2 11.5 %fusion.3 = f32[8,32,64,256]{3,2,1,0:T(8,128)} fusion(bf16[8,32,64,256]{3,2,1,0:T(8,128)(2,1)} %collective-permute-done, bf16[8,32,64,256]{3,2,1,0:T(8,128)(2,1)S(1)} %copy-done.1, s32[]{:T(128)S(6)} %select_n.56), kind=kOutput, calls=%fused_computation.6 | convolution fusion | flops 536870912 | bytes 29360132 | tf_op jit(solution)/shard_map/pqab,pqbc->pqac/dot_general | solution.py:49
  248.7 32.1 %collective-permute-done.2 = bf16[8,32,64,256]{3,2,1,0:T(8,128)(2,1)} collective-permute-done((bf16[8,32,64,256]{3,2,1,0:T(8,128)(2,1)}, bf16[8,32,64,256]{3,2,1,0:T(8,128)(2,1)}, u32[]{:S(2)}, u32[]{:S(2)}) %collective-permute-start.2) | collective-permute-done | bytes 8388640 | tf_op jit(solution)/shard_map/ppermute | solution.py:17
  280.9 24.3 %add_convert_fusion = bf16[8,32,64,256]{3,2,1,0:T(8,128)(2,1)} fusion(f32[8,32,64,256]{3,2,1,0:T(8,128)} %fusion.1, f32[8,32,64,256]{3,2,1,0:T(8,128)} %fusion.5, f32[8,32,64,256]{3,2,1,0:T(8,128)} %fusion.3, bf16[8,32,64,256]{3,2,1,0:T(8,128)(2,1)} %collective-permute-done.2, bf16[8,32,64,256]{3,2,1,0:T(8,128)(2,1)} %broadcast_select_fusion, s32[]{:T(128)S(6)} %select_n.60), kind=kOutput, calls=%fused_computation.1 | convolution fusion | flops 553648128 | bytes 71303168 | tf_op jit(solution)/shard_map/pqab,pqbc->pqac/dot_general | solution.py:49
  305.2 1.7 fusion.11
  306.9 1.5 fusion.12
  308.4 2.8 fusion.13
  311.2 3.0 fusion.14
  314.2 3.0 fusion.15
  317.2 3.2 fusion.16
  320.4 2.8 fusion.17
  323.2 2.8 fusion.18
  326.0 1.8 fusion.19
  327.8 1.8 fusion.20
  329.6 1.8 fusion.21
  331.5 1.8 fusion.22
  333.3 1.8 fusion.23
  335.1 1.8 fusion.24
  336.9 1.9 fusion.25
  338.8 1.8 fusion.26
  340.5 1.8 fusion.27
  342.4 1.8 fusion.28
  344.2 1.8 fusion.29
  346.0 1.8 fusion.30
  347.8 1.8 fusion.31
  349.6 1.8 fusion.32
  351.4 1.8 fusion.33
  353.2 1.8 fusion.34
  355.0 1.8 fusion.35
  356.8 1.8 fusion.36
  358.6 1.8 fusion.37
  360.4 1.8 fusion.38
  362.2 1.8 fusion.39
  364.0 1.8 fusion.40
  365.8 1.8 fusion.41
  367.6 1.8 fusion.42
  369.4 22.2 %bitcast_add_fusion = f32[8,256,256]{2,1,0:T(8,128)} fusion(f32[8,256,256]{1,2,0:T(8,128)S(1)} %fusion.11, f32[8,256,256]{1,2,0:T(8,128)S(1)} %fusion.12, f32[8,256,256]{1,2,0:T(8,128)} %fusion.13, f32[8,256,256]{1,2,0:T(8,128)} %fusion.14, f32[8,256,256]{1,2,0:T(8,128)} %fusion.15, f32[8,256,256]{1,2,0:T(8,128)} %fusion.16, f32[8,256,256]{1,2,0:T(8,128)} %fusion.17, ...), kind=kOutput, calls=%fused_computation.10 | convolution fusion | flops 100663296 | bytes 70008832 | tf_op jit(solution)/shard_map/pab,pbc->pac/dot_general | solution.py:42
  391.6 35.2 %reduce-scatter.2.cloned.1.call-done = f32[8,64,256]{2,1,0:T(8,128)} async-done(((f32[8,256,256]{2,1,0:T(8,128)}), f32[8,64,256]{2,1,0:T(8,128)}) %reduce-scatter.2.cloned.1.call-update) | async-done | bytes 524304 | tf_op jit(solution)/shard_map/reduce_scatter | solution.py:64
  426.8 2.1 fusion.9
  (30 shorter events, 3.5 us)
Async XLA Ops:
  6.5 362.9 %copy-start = (bf16[8,256,256]{2,1,0:T(8,128)(2,1)S(1)}, bf16[8,256,256]{2,1,0:T(8,128)(2,1)}, u32[]{:S(2)}) copy-start(bf16[8,256,256]{2,1,0:T(8,128)(2,1)} %param.9) | copy-start | bytes 3145732
  6.5 188.6 %all-gather.2.cloned.1.call-start = ((), (), s32[]{:S(2)}) async-start(), calls=%async_computation.1 | async-start | bytes 2359296 | tf_op jit(solution)/shard_map/all_gather | solution.py:36
  6.5 181.1 %collective-permute-start.1 = (bf16[8,32,64,256]{3,2,1,0:T(8,128)(2,1)}, bf16[8,32,64,256]{3,2,1,0:T(8,128)(2,1)}, u32[]{:S(2)}, u32[]{:S(2)}) collective-permute-start(bf16[8,32,64,256]{3,2,1,0:T(8,128)(2,1)} %param.11), channel_id=1, source_target_pairs={{0,1},{1,2},{2,3},{3,0},{4,5},{5,6},{6,7},{7,4},{8,9},{9,10},{10,1... | collective-permute-start | bytes 25165832 | tf_op jit(solution)/shard_map/ppermute | solution.py:17
  7.0 230.2 %collective-permute-start = (bf16[8,32,64,256]{3,2,1,0:T(8,128)(2,1)}, bf16[8,32,64,256]{3,2,1,0:T(8,128)(2,1)}, u32[]{:S(2)}, u32[]{:S(2)}) collective-permute-start(bf16[8,32,64,256]{3,2,1,0:T(8,128)(2,1)} %param.11), channel_id=1, source_target_pairs={{0,3},{1,0},{2,1},{3,2},{4,7},{5,4},{6,5},{7,6},{8,11},{9,8},{10,9... | collective-permute-start | bytes 25165832 | tf_op jit(solution)/shard_map/ppermute | solution.py:19
  12.2 414.6 %reduce-scatter.2.cloned.1.call-start = ((), (), s32[]{:S(2)}) async-start(), calls=%async_computation.2 | async-start | bytes 2621440 | tf_op jit(solution)/shard_map/reduce_scatter | solution.py:64
  187.7 93.2 %collective-permute-start.2 = (bf16[8,32,64,256]{3,2,1,0:T(8,128)(2,1)}, bf16[8,32,64,256]{3,2,1,0:T(8,128)(2,1)}, u32[]{:S(2)}, u32[]{:S(2)}) collective-permute-start(bf16[8,32,64,256]{3,2,1,0:T(8,128)(2,1)} %collective-permute-done.1), channel_id=1, source_target_pairs={{0,1},{1,2},{2,3},{3,0},{4,5},{5,6},{6,7},{7,4},{8,9},{9,10},{10,1... | collective-permute-start | bytes 25165832 | tf_op jit(solution)/shard_map/ppermute | solution.py:17
  212.7 12.9 %copy-start.1 = (bf16[8,32,64,256]{3,2,1,0:T(8,128)(2,1)S(1)}, bf16[8,32,64,256]{3,2,1,0:T(8,128)(2,1)}, u32[]{:S(2)}) copy-start(bf16[8,32,64,256]{3,2,1,0:T(8,128)(2,1)} %broadcast_select_fusion) | copy-start | bytes 25165828
  305.2 15.2 %slice-start = ((s8[8388608]{0:T(1024)(128)(4,1)}), s8[4194304]{0:T(1024)(128)(4,1)S(1)}, s32[]{:S(2)}) async-start(s8[8388608]{0:T(1024)(128)(4,1)} %bitcast.391), calls=%async_computation.3 | async-start | bytes 8388608
  311.2 9.2 %slice-start.1 = ((s8[8388608]{0:T(1024)(128)(4,1)}), s8[4194304]{0:T(1024)(128)(4,1)S(1)}, s32[]{:S(2)}) async-start(s8[8388608]{0:T(1024)(128)(4,1)} %bitcast.391), calls=%async_computation.4 | async-start | bytes 8388608
  314.2 11.8 %copy-start.2 = (bf16[8,32,64,256]{3,2,1,0:T(8,128)(2,1)S(1)}, bf16[8,32,64,256]{3,2,1,0:T(8,128)(2,1)}, u32[]{:S(2)}) copy-start(bf16[8,32,64,256]{3,2,1,0:T(8,128)(2,1)} %add_convert_fusion) | copy-start | bytes 25165828
  365.8 3.6 copy-start.3
  391.6 35.2 %copy-start.4 = (bf16[8,64,256]{2,1,0:T(8,128)(2,1)S(1)}, bf16[8,64,256]{2,1,0:T(8,128)(2,1)}, u32[]{:S(2)}) copy-start(bf16[8,64,256]{2,1,0:T(8,128)(2,1)} %param.10) | copy-start | bytes 786436
Sparse Core Ops, SparseCore 0:
  12.4 51.1 all-gather.1
  391.7 35.0 reduce-scatter.1
